TPU v7x, 32 devices: a whole 2x2x4 slice. The times are simulated.
32 devices in a mesh: section: 4 (over y, x), tp: 8 (over z, core).
Axes of the slice: x: 2, y: 2, z: 4, core: 2. Of those that a mesh axis runs over, the one named last changes fastest.
Arguments:
- awaiting_arrivals: bfloat16 [4, 8, 25, 1920], P('section', 'tp'), may hold values from -6 to 6
- label_numbers: int32 [5, 8], replicated, may hold values from 0 to 1000
- drawn_coarse_codes: int32 [1, 8, 30], replicated, may hold values from 0 to 4095
- discrete_prototypes: float32 [4096, 32], replicated, may hold values from -6 to 6
- code_raising_operator: bfloat16 [32, 1920], replicated, may hold values from -1 to 1
- placement_tier_features: bfloat16 [25, 1920], replicated, may hold values from -3 to 3
- label_feature_rows: bfloat16 [1001, 1920], P(None, 'tp'), may hold values from -6 to 6
- conditioned_gain_mapping: bfloat16 [4, 1920, 3, 1920], P('section', None, None, 'tp'), may hold values from -0.125 to 0.125
- conditioned_shift_addend: float32 [4, 3, 1920], P('section', None, 'tp'), may hold values from -3 to 3
- question_answer_operator: bfloat16 [4, 1920, 3, 1920], P('section', None, None, 'tp'), may hold values from -0.125 to 0.125
- mixing_return_operator: bfloat16 [4, 1920, 1920], P('section', None, 'tp'), may hold values from -0.125 to 0.125
- focus_sharpness_exponents: float32 [4, 30], P('section'), may hold values from 1 to 5.5
- prior_resolution_probes: bfloat16 [4, 2, 8, 30, 1920], P('section', None, 'tp'), may hold values from -0.75 to 0.75
- prior_resolution_answers: bfloat16 [4, 2, 8, 30, 1920], P('section', None, 'tp'), may hold values from -6 to 6
Outputs:
- section_out: bfloat16 [4, 2, 8, 25, 1920], P('section', None, 'tp')
Inputs may be any that keep to these rules, and one draw needn't show every extreme that they name: `drawn_coarse_codes`: codebook indices of the maps of sides 1 to 4 of each image, one map after another, each row by row. `label_numbers`: class of each image; row r belongs to the micro-batch r - 4.
All inputs are finite; a program needn't handle non-finite values.
Results may differ from a plain program's by a relative error of at most 0.0151.
Values may be sent and summed in bfloat16 or wider, within the bound.
No kernel may reach another device: no remote copies, remote signals or barrier semaphores. Data moves between devices by JAX's collectives and lax.ppermute only.
A program may use at most 128 MiB of HBM per device.

v0:
```python
import jax
import jax.numpy as jnp
from jax import lax
from jax.sharding import PartitionSpec as P

FOCUS_GROUPS = 30
HEAD_DIM = 64
SIDE = 5
LOG_CAP = 4.605170185988092


def shifted(value, axis, steps):
    count = lax.axis_size(axis)
    first, last = (max(0, -steps), min(count, count - steps))
    return lax.ppermute(value, axis, [(source, source + steps) for source in range(first, last)])


def crossing_matrix(target, coarse):
    fine_index = jnp.arange(target, dtype=jnp.float32)
    coarse_index = jnp.arange(coarse, dtype=jnp.float32)
    begins = jnp.maximum(fine_index[:, None] / target, coarse_index[None, :] / coarse)
    finish = jnp.minimum(
        (fine_index[:, None] + 1.0) / target, (coarse_index[None, :] + 1.0) / coarse
    )
    return jnp.maximum(finish - begins, 0.0) * target


def resampler():
    blocks = []
    for coarse in range(1, SIDE):
        crossing = crossing_matrix(SIDE, coarse)
        blocks.append(
            (crossing[:, None, :, None] * crossing[None, :, None, :]).reshape(
                SIDE * SIDE, coarse * coarse
            )
        )
    return jnp.concatenate(blocks, axis=1)


def embed(
    drawn_coarse_codes,
    discrete_prototypes,
    code_raising_operator,
    placement_tier_features,
    resample_table,
):
    looked_up = discrete_prototypes[drawn_coarse_codes]
    mapped = jnp.einsum(
        "tc,nicv->nitv", resample_table, looked_up, precision=lax.Precision.HIGHEST
    ).astype(jnp.bfloat16)
    leading = mapped.shape[:3]
    projected_rows = jnp.dot(
        mapped.reshape(-1, mapped.shape[3]),
        code_raising_operator,
        preferred_element_type=jnp.float32,
    )
    projected_rows = projected_rows.reshape(leading + (code_raising_operator.shape[1],))
    return (projected_rows + placement_tier_features.astype(jnp.float32)).astype(jnp.bfloat16)


def norm_mod(latent_stream, scale_term, offset_term):
    widened = latent_stream.astype(jnp.float32)
    average = jnp.mean(widened, axis=-1, keepdims=True)
    centred = widened - average
    spread = jnp.mean(centred * centred, axis=-1, keepdims=True)
    normed = (
        centred * lax.rsqrt(spread + 1e-06) * (1.0 + scale_term[:, None, :])
        + offset_term[:, None, :]
    )
    return normed.astype(jnp.bfloat16)


def attention(qkv_cols, log_scale, cached_keys, cached_values):
    qkv = lax.all_to_all(qkv_cols, "tp", split_axis=0, concat_axis=3, tiled=True)
    images = qkv.shape[0]
    count = qkv.shape[1]
    widened = qkv.astype(jnp.float32)
    query = widened[:, :, 0].reshape(images, count, FOCUS_GROUPS, HEAD_DIM)
    new_keys = widened[:, :, 1].reshape(images, count, FOCUS_GROUPS, HEAD_DIM)
    new_values = qkv[:, :, 2].reshape(images, count, FOCUS_GROUPS, HEAD_DIM)
    head_mult = jnp.exp(jnp.minimum(log_scale, LOG_CAP))
    query = (
        query
        * lax.rsqrt(jnp.sum(query * query, axis=-1, keepdims=True) + 1e-06)
        * head_mult[:, None]
    )
    new_keys = new_keys * lax.rsqrt(jnp.sum(new_keys * new_keys, axis=-1, keepdims=True) + 1e-06)
    all_keys = jnp.concatenate(
        [cached_keys.astype(jnp.float32).reshape(images, -1, FOCUS_GROUPS, HEAD_DIM), new_keys],
        axis=1,
    )
    all_values = jnp.concatenate(
        [cached_values.reshape(images, -1, FOCUS_GROUPS, HEAD_DIM), new_values], axis=1
    )
    scores = jnp.einsum("iqhd,ikhd->ihqk", query, all_keys, precision=lax.Precision.HIGHEST)
    maximum = jnp.max(scores, axis=-1, keepdims=True)
    weights = jnp.exp(scores - maximum)
    probabilities = (weights / jnp.sum(weights, axis=-1, keepdims=True)).astype(jnp.bfloat16)
    mixed = jnp.einsum(
        "ihqk,ikhd->iqhd", probabilities, all_values, preferred_element_type=jnp.float32
    )
    return mixed.reshape(images, count, FOCUS_GROUPS * HEAD_DIM).astype(jnp.bfloat16)


def project_out(attended, out_matrix):
    return jnp.dot(
        lax.all_gather(attended, "tp", axis=0, tiled=True),
        out_matrix,
        preferred_element_type=jnp.float32,
    )


def pass_on(latent_stream):
    return shifted(latent_stream, "section", 1)


def local(
    awaiting_arrivals,
    label_numbers,
    drawn_coarse_codes,
    discrete_prototypes,
    code_raising_operator,
    placement_tier_features,
    label_feature_rows,
    conditioned_gain_mapping,
    conditioned_shift_addend,
    question_answer_operator,
    mixing_return_operator,
    focus_sharpness_exponents,
    prior_resolution_probes,
    prior_resolution_answers,
):
    sections = lax.axis_size("section")
    section_at = lax.axis_index("section")
    group_index = lax.axis_index("tp")
    moments = prior_resolution_probes.shape[1]
    width = question_answer_operator.shape[1]
    column_width = question_answer_operator.shape[3]
    images = drawn_coarse_codes.shape[1]
    resident_pictures = awaiting_arrivals.shape[1]
    class_rows = lax.dynamic_slice_in_dim(label_numbers, sections - 1 - section_at, moments, 0)
    class_part = jnp.take(label_feature_rows, class_rows, axis=0)
    activated_part = jax.nn.silu(class_part.astype(jnp.float32)).astype(jnp.bfloat16)
    gated_response = lax.all_gather(activated_part, "tp", axis=2, tiled=True)
    flat_active = gated_response.reshape(moments * images, width)
    inner_block = 0
    local_mod = conditioned_gain_mapping[inner_block].reshape(width, 3 * column_width)
    modulated = jnp.dot(flat_active, local_mod, preferred_element_type=jnp.float32)
    mod_list = [
        modulated.reshape(moments, images, 3, column_width) + conditioned_shift_addend[inner_block]
    ]
    mod_cols = jnp.stack(mod_list)
    resample_table = resampler()
    emitted = []
    mod_rows = lax.all_to_all(mod_cols, "tp", split_axis=2, concat_axis=4, tiled=True)
    own_tokens = lax.dynamic_slice_in_dim(
        drawn_coarse_codes, group_index * resident_pictures, resident_pictures, 1
    )
    entering = embed(
        own_tokens,
        discrete_prototypes,
        code_raising_operator,
        placement_tier_features,
        resample_table,
    )
    passed_along_activation = awaiting_arrivals[0]
    for clock_tick in range(moments):
        latent_stream = passed_along_activation
        inner_block = 0
        modulation = mod_rows[inner_block, clock_tick]
        normed = norm_mod(latent_stream, modulation[:, 1], modulation[:, 2])
        local_qkv = question_answer_operator[inner_block].reshape(width, 3 * column_width)

        def body_product(portion, offset, local_qkv=local_qkv):
            return jnp.dot(portion, local_qkv, preferred_element_type=jnp.float32).astype(
                jnp.bfloat16
            )

        qkv_cols = body_product(lax.all_gather(normed, "tp", axis=0, tiled=True), jnp.int32(0))
        qkv_cols = qkv_cols.reshape(qkv_cols.shape[0], qkv_cols.shape[1], 3, column_width)
        attended = attention(
            qkv_cols,
            focus_sharpness_exponents[inner_block],
            prior_resolution_probes[inner_block, clock_tick],
            prior_resolution_answers[inner_block, clock_tick],
        )
        projected_cols = project_out(attended, mixing_return_operator[inner_block]).astype(
            jnp.bfloat16
        )
        projected = lax.all_to_all(projected_cols, "tp", split_axis=0, concat_axis=2, tiled=True)
        latent_stream = (
            latent_stream.astype(jnp.float32)
            + modulation[:, 0][:, None, :] * projected.astype(jnp.float32)
        ).astype(jnp.bfloat16)
        emitted.append(latent_stream)
        if clock_tick + 1 < moments:
            arrived = pass_on(latent_stream)
            passed_along_activation = jnp.where(section_at == 0, entering[clock_tick], arrived)
    result = jnp.stack(emitted)
    return result[None]


def solution(mesh):
    in_specs = (
        P("section", "tp", None, None),
        P(),
        P(),
        P(),
        P(),
        P(),
        P(None, "tp"),
        P("section", None, None, "tp"),
        P("section", None, "tp"),
        P("section", None, None, "tp"),
        P("section", None, "tp"),
        P("section", None),
        P("section", None, "tp", None, None),
        P("section", None, "tp", None, None),
    )
    out_specs = P("section", None, "tp", None, None)
    return jax.shard_map(local, mesh=mesh, in_specs=in_specs, out_specs=out_specs, check_vma=False)
```

profile of v0, /device:TPU:4, one launch (start us, length us, event | category | flops | bytes accessed | tf_op | source)
XLA Modules:
  0.0 244.2 jit_solution(13599707762112273153)
XLA Ops:
  0.9 1.2 copy.162
  3.0 16.4 %all_gather.15 = bf16[2,8,1920]{1,0,2:T(2,128)(2,1)S(1)} all-gather(bf16[2,8,240]{1,0,2:T(2,128)(2,1)S(1)} %copy.163), channel_id=1, replica_groups=mesh['section'=4,'tp'=8] {'tp'}, dimensions={2}, use_global_device_ids=true | all-gather | bytes 69120 | tf_op jit(solution)/shard_map/all_gather | solution.py:144
  20.1 2.9 %fusion.17 = f32[1,2,8,3,240]{4,2,3,1,0:T(8,128)S(1)} fusion(bf16[1,1920,3,240]{1,3,2,0:T(8,128)(2,1)} %param.21, bf16[2,8,1920,1]{1,0,2,3:T(2,128)(2,1)S(1)} %bitcast.178, f32[3,240]{1,0:T(4,128)S(1)} %bitcast.180), kind=kOutput, calls=%fused_computation.24 | convolution fusion | flops 44248320 | bytes 2875200 | tf_op jit(solution)/shard_map/dot_general | solution.py:148
  23.7 5.1 %all-to-all-start = ((f32[1,2,8,3,240]{4,1,3,0,2:T(2,128)}), f32[1,2,8,3,240]{4,1,3,0,2:T(2,128)S(1)}, u32[]{:S(2)}, u32[]{:S(2)}) async-start(f32[1,2,8,3,240]{4,1,3,0,2:T(2,128)} %copy.165), calls=%async_computation | async-start | bytes 98304 | tf_op jit(solution)/shard_map/all_to_all | solution.py:155
  29.2 1.5 convert_reduce_fusion.1
  32.4 2.8 %slice_reduce_fusion = (bf16[30,1920]{1,0:T(8,128)(2,1)}, bf16[30,1920]{1,0:T(8,128)(2,1)}) fusion(bf16[1,2,1,30,1920]{4,1,3,2,0:T(2,128)(2,1)} %param.27), kind=kLoop, calls=%fused_computation.77 | loop fusion | bytes 460800 | tf_op jit(solution)/shard_map/slice | solution.py:185
  36.7 17.0 %all_gather.16 = bf16[8,25,1920]{2,1,0:T(8,128)(2,1)S(1)} all-gather(bf16[1,25,1920]{2,1,0:T(8,128)(2,1)S(1)} %fusion.43), channel_id=1, replica_groups=mesh['section'=4,'tp'=8] {'tp'}, dimensions={0}, use_global_device_ids=true | all-gather | bytes 864000 | tf_op jit(solution)/shard_map/all_gather | solution.py:179
  53.6 1.8 convolution_convert_fusion.1
  55.4 1.7 reshape.1148
  58.0 5.2 %all-to-all-start.1 = ((bf16[8,25,3,240]{3,1,2,0:T(8,128)(2,1)}), bf16[8,25,3,240]{3,1,2,0:T(8,128)(2,1)}, u32[]{:S(2)}, u32[]{:S(2)}) async-start(bf16[8,25,3,240]{3,1,2,0:T(8,128)(2,1)} %copy.169), calls=%async_computation.1 | async-start | bytes 786432 | tf_op jit(solution)/shard_map/all_to_all | solution.py:74
  67.0 3.0 %copy.180 = f32[4096,32]{1,0:T(8,128)} copy(f32[4096,32]{0,1:T(8,128)} %param.17) | data formatting | bytes 1048576 | tf_op args[3]
  73.9 2.8 %gather_fusion.1 = f32[30,32]{1,0:T(8,128)} fusion(f32[4096,32]{1,0:T(8,128)} %copy.180, s32[1024]{0:T(1024)S(1)} %pad_clamp_fusion), kind=kCustom, calls=%fused_computation.1 | custom fusion | bytes 7800 | tf_op jit(solution)/shard_map/gather | solution.py:47
  82.2 1.4 copy.173
  83.6 1.8 copy_multiply_fusion.1
  86.5 1.7 slice_multiply_fusion.1
  88.1 1.9 mul.390
  91.4 2.8 %fusion.24 = f32[30,25,55]{2,1,0:T(8,128)S(1)} fusion(f32[1,25,30,64]{3,1,2,0:T(8,128)} %copy_multiply_fusion.1, f32[1,30,30,64]{3,1,2,0:T(8,128)} %copy.175, f32[25,30,64]{2,1,0:T(8,128)S(1)} %multiply_multiply_fusion.1), kind=kOutput, calls=%fused_computation.31 | convolution fusion | flops 31785600 | bytes 779400 | tf_op jit(solution)/shard_map/iqhd,ikhd->ihqk/dot_general | solution.py:95
  95.5 1.7 copy.172
  97.2 3.5 %fusion.12 = bf16[1,25,30,64]{3,1,2,0:T(8,128)(2,1)} fusion(bf16[1,25,30,64]{3,1,2,0:T(8,128)(2,1)} %copy.172, bf16[1,30,30,64]{3,1,2,0:T(8,128)(2,1)} %copy.171, f32[30,25]{1,0:T(8,128)S(1)} %fusion.73, f32[30,25,55]{2,1,0:T(8,128)S(1)} %fusion.24), kind=kOutput, calls=%fused_computation.19 | convolution fusion | flops 5874954 | bytes 475200 | tf_op jit(solution)/shard_map/ihqk,ikhd->iqhd/dot_general | solution.py:99
  102.0 17.0 %all_gather.17 = bf16[8,25,1920]{2,1,0:T(8,128)(2,1)S(1)} all-gather(bf16[1,25,1920]{2,1,0:T(8,128)(2,1)S(1)} %convert_element_type.264), channel_id=1, replica_groups=mesh['section'=4,'tp'=8] {'tp'}, dimensions={0}, use_global_device_ids=true | all-gather | bytes 864000 | tf_op jit(solution)/shard_map/all_gather | solution.py:107
  119.0 2.3 convolution_convert_fusion.5
  121.2 5.2 %all-to-all-start.2 = ((bf16[8,25,240]{2,1,0:T(8,128)(2,1)}), bf16[8,25,240]{2,1,0:T(8,128)(2,1)S(1)}, u32[]{:S(2)}, u32[]{:S(2)}) async-start(bf16[8,25,240]{2,1,0:T(8,128)(2,1)} %convolution_convert_fusion.5), calls=%async_computation.2 | async-start | bytes 262144 | tf_op jit(solution)/shard_map/all_to_all | solution.py:190
  126.7 6.5 %all-to-all-done.2 = bf16[8,25,240]{2,1,0:T(8,128)(2,1)S(1)} async-done(((bf16[8,25,240]{2,1,0:T(8,128)(2,1)}), bf16[8,25,240]{2,1,0:T(8,128)(2,1)S(1)}, u32[]{:S(2)}, u32[]{:S(2)}) %all-to-all-start.2) | async-done | bytes 96032 | tf_op jit(solution)/shard_map/all_to_all | solution.py:190
  133.6 3.4 %collective-permute-start = (bf16[1,25,1920]{2,1,0:T(8,128)(2,1)S(1)}, bf16[1,25,1920]{2,1,0:T(8,128)(2,1)S(1)}, u32[]{:S(2)}, u32[]{:S(2)}) collective-permute-start(bf16[1,25,1920]{2,1,0:T(8,128)(2,1)S(1)} %fusion.44), channel_id=1, source_target_pairs={{0,8},{8,16},{16,24},{1,9},{9,17},{17,25},{2,10},{10,18},{18,26},{... | collective-permute-start | bytes 288008 | tf_op jit(solution)/shard_map/ppermute | solution.py:15
  137.6 3.6 %collective-permute-done = bf16[1,25,1920]{2,1,0:T(8,128)(2,1)S(1)} collective-permute-done((bf16[1,25,1920]{2,1,0:T(8,128)(2,1)S(1)}, bf16[1,25,1920]{2,1,0:T(8,128)(2,1)S(1)}, u32[]{:S(2)}, u32[]{:S(2)}) %collective-permute-start) | collective-permute-done | bytes 96032 | tf_op jit(solution)/shard_map/ppermute | solution.py:15
  141.2 1.3 fusion.74
  142.9 16.3 %all_gather.18 = bf16[8,25,1920]{2,1,0:T(8,128)(2,1)S(1)} all-gather(bf16[1,25,1920]{2,1,0:T(8,128)(2,1)S(1)} %add_convert_fusion.1), channel_id=1, replica_groups=mesh['section'=4,'tp'=8] {'tp'}, dimensions={0}, use_global_device_ids=true | all-gather | bytes 864000 | tf_op jit(solution)/shard_map/all_gather | solution.py:179
  159.2 1.8 convolution_convert_fusion
  161.0 2.4 reshape.1151
  163.4 1.8 copy.187
  165.2 4.3 %all-to-all-start.3 = ((bf16[8,25,3,240]{3,1,2,0:T(8,128)(2,1)}), bf16[8,25,3,240]{3,1,2,0:T(8,128)(2,1)}, u32[]{:S(2)}, u32[]{:S(2)}) async-start(bf16[8,25,3,240]{3,1,2,0:T(8,128)(2,1)} %copy.187), calls=%async_computation.3 | async-start | bytes 786432 | tf_op jit(solution)/shard_map/all_to_all | solution.py:74
  169.5 2.0 reshape.1119
  171.5 2.1 copy.193
  174.5 1.7 copy.189
  177.1 4.7 %all-to-all-done.3 = bf16[8,25,3,240]{3,1,2,0:T(8,128)(2,1)} async-done(((bf16[8,25,3,240]{3,1,2,0:T(8,128)(2,1)}), bf16[8,25,3,240]{3,1,2,0:T(8,128)(2,1)}, u32[]{:S(2)}, u32[]{:S(2)}) %all-to-all-start.3) | async-done | bytes 288032 | tf_op jit(solution)/shard_map/all_to_all | solution.py:74
  181.8 1.9 copy.188
  183.7 1.4 all_to_all.65
  186.8 1.9 mul.431
  189.9 1.9 reshape_squeeze.39
  191.8 1.9 reshape_squeeze.40
  196.4 1.3 copy_multiply_fusion
  198.8 2.7 %fusion.27 = f32[30,25,55]{2,1,0:T(8,128)S(1)} fusion(f32[1,25,30,64]{3,1,2,0:T(8,128)S(1)} %copy_multiply_fusion, f32[1,30,30,64]{3,1,2,0:T(8,128)} %copy.193, f32[25,30,64]{2,1,0:T(8,128)S(1)} %multiply_multiply_fusion), kind=kOutput, calls=%fused_computation.35 | convolution fusion | flops 31785600 | bytes 779400 | tf_op jit(solution)/shard_map/iqhd,ikhd->ihqk/dot_general | solution.py:95
  203.6 3.8 %fusion.13 = bf16[1,25,30,64]{3,1,2,0:T(8,128)(2,1)} fusion(bf16[1,25,30,64]{3,1,2,0:T(8,128)(2,1)} %copy.190, bf16[1,30,30,64]{3,1,2,0:T(8,128)(2,1)} %copy.189, f32[30,25]{1,0:T(8,128)S(1)} %fusion.75, f32[30,25,55]{2,1,0:T(8,128)} %copy-done.5), kind=kOutput, calls=%fused_computation.20 | convolution fusion | flops 5874954 | bytes 475200 | tf_op jit(solution)/shard_map/ihqk,ikhd->iqhd/dot_general | solution.py:99
  207.4 1.7 copy.195
  210.3 16.2 %all_gather.19 = bf16[8,25,1920]{2,1,0:T(8,128)(2,1)S(1)} all-gather(bf16[1,25,1920]{2,1,0:T(8,128)(2,1)S(1)} %convert_element_type.289), channel_id=1, replica_groups=mesh['section'=4,'tp'=8] {'tp'}, dimensions={0}, use_global_device_ids=true | all-gather | bytes 864000 | tf_op jit(solution)/shard_map/all_gather | solution.py:107
  226.5 2.3 convolution_convert_fusion.4
  228.8 4.0 %all-to-all-start.4 = ((bf16[8,25,240]{2,1,0:T(8,128)(2,1)}), bf16[8,25,240]{2,1,0:T(8,128)(2,1)}, u32[]{:S(2)}, u32[]{:S(2)}) async-start(bf16[8,25,240]{2,1,0:T(8,128)(2,1)} %convolution_convert_fusion.4), calls=%async_computation.4 | async-start | bytes 262144 | tf_op jit(solution)/shard_map/all_to_all | solution.py:190
  233.5 6.1 %all-to-all-done.4 = bf16[8,25,240]{2,1,0:T(8,128)(2,1)} async-done(((bf16[8,25,240]{2,1,0:T(8,128)(2,1)}), bf16[8,25,240]{2,1,0:T(8,128)(2,1)}, u32[]{:S(2)}, u32[]{:S(2)}) %all-to-all-start.4) | async-done | bytes 96032 | tf_op jit(solution)/shard_map/all_to_all | solution.py:190
  (142 shorter events, 44.2 us)
Async XLA Ops:
  0.0 53.6 %copy-start = (bf16[1,1920,3,240]{1,3,2,0:T(8,128)(2,1)S(1)}, bf16[1,1920,3,240]{1,3,2,0:T(8,128)(2,1)}, u32[]{:S(2)}) copy-start(bf16[1,1920,3,240]{1,3,2,0:T(8,128)(2,1)} %param.23) | copy-start | bytes 8294404
  2.2 26.7 %copy-start.3 = (bf16[1,1,25,1920]{3,2,1,0:T(8,128)(2,1)S(1)}, bf16[1,1,25,1920]{3,2,1,0:T(8,128)(2,1)}, u32[]{:S(2)}) copy-start(bf16[1,1,25,1920]{3,2,1,0:T(8,128)(2,1)} %param.14) | copy-start | bytes 288004
  2.8 26.5 %copy-start.7 = (bf16[1,2,1,30,1920]{4,1,3,2,0:T(2,128)(2,1)S(1)}, bf16[1,2,1,30,1920]{4,1,3,2,0:T(2,128)(2,1)}, u32[]{:S(2)}) copy-start(bf16[1,2,1,30,1920]{4,1,3,2,0:T(2,128)(2,1)} %param.26) | copy-start | bytes 691204
  23.7 11.5 %all-to-all-start = ((f32[1,2,8,3,240]{4,1,3,0,2:T(2,128)}), f32[1,2,8,3,240]{4,1,3,0,2:T(2,128)S(1)}, u32[]{:S(2)}, u32[]{:S(2)}) async-start(f32[1,2,8,3,240]{4,1,3,0,2:T(2,128)} %copy.165), calls=%async_computation | async-start | bytes 98304 | tf_op jit(solution)/shard_map/all_to_all | solution.py:155
  58.0 18.7 %all-to-all-start.1 = ((bf16[8,25,3,240]{3,1,2,0:T(8,128)(2,1)}), bf16[8,25,3,240]{3,1,2,0:T(8,128)(2,1)}, u32[]{:S(2)}, u32[]{:S(2)}) async-start(bf16[8,25,3,240]{3,1,2,0:T(8,128)(2,1)} %copy.169), calls=%async_computation.1 | async-start | bytes 786432 | tf_op jit(solution)/shard_map/all_to_all | solution.py:74
  64.0 6.7 %copy-start.9 = (f32[5,5,3,3]{1,0,3,2:T(8,128)S(1)}, f32[5,5,3,3]{1,0,3,2:T(8,128)}, u32[]{:S(2)}) copy-start(f32[5,5,3,3]{1,0,3,2:T(8,128)} %broadcast_multiply_fusion.1) | copy-start | bytes 2704
  64.0 7.5 %copy-start.12 = (f32[5,5,2,2]{1,0,3,2:T(8,128)S(1)}, f32[5,5,2,2]{1,0,3,2:T(8,128)}, u32[]{:S(2)}) copy-start(f32[5,5,2,2]{1,0,3,2:T(8,128)} %broadcast_multiply_fusion.2) | copy-start | bytes 1204
  64.0 8.3 %copy-start.19 = (f32[5]{0:T(128)S(1)}, f32[5]{0:T(128)}, u32[]{:S(2)}) copy-start(f32[5]{0:T(128)} %maximum_multiply_fusion.3) | copy-start | bytes 64
  64.0 12.7 %copy-start.20 = (f32[1,30]{1,0:T(1,128)S(1)}, f32[1,30]{1,0:T(1,128)}, u32[]{:S(2)}) copy-start(f32[1,30]{1,0:T(1,128)} %param.25) | copy-start | bytes 364
  78.4 9.8 %copy-start.1 = (bf16[1,25,3,1920]{3,1,2,0:T(8,128)(2,1)}, bf16[1,25,3,1920]{3,1,2,0:T(8,128)(2,1)S(1)}, u32[]{:S(2)}) copy-start(bf16[1,25,3,1920]{3,1,2,0:T(8,128)(2,1)S(1)} %all_to_all.60) | copy-start | bytes 864004
  90.0 4.6 %slice-start = ((bf16[1,25,3,1920]{3,1,2,0:T(8,128)(2,1)}), bf16[1,25,1,1920]{3,1,2,0:T(8,128)(2,1)S(1)}, s32[]{:S(2)}) async-start(bf16[1,25,3,1920]{3,1,2,0:T(8,128)(2,1)} %copy-done.1), calls=%async_computation.5 | async-start | bytes 245760 | tf_op jit(solution)/shard_map/slice | solution.py:80
  100.6 25.8 %copy-start.13 = (f32[30,32]{1,0:T(8,128)S(1)}, f32[30,32]{1,0:T(8,128)}, u32[]{:S(2)}) copy-start(f32[30,32]{1,0:T(8,128)} %gather_fusion.1) | copy-start | bytes 11524
  100.6 25.8 %copy-start.14 = (f32[25,9]{1,0:T(8,128)S(1)}, f32[25,9]{1,0:T(8,128)}, u32[]{:S(2)}) copy-start(f32[25,9]{1,0:T(8,128)} %copy.183) | copy-start | bytes 2704
  100.6 25.8 %copy-start.15 = (f32[25,4]{1,0:T(8,128)S(1)}, f32[25,4]{1,0:T(8,128)}, u32[]{:S(2)}) copy-start(f32[25,4]{1,0:T(8,128)} %copy.182) | copy-start | bytes 1204
  100.6 25.8 %copy-start.16 = (f32[25,1]{1,0:T(8,128)S(1)}, f32[25,1]{1,0:T(8,128)}, u32[]{:S(2)}) copy-start(f32[25,1]{1,0:T(8,128)} %copy.181) | copy-start | bytes 304
  100.6 25.8 %copy-start.17 = (f32[25,16]{1,0:T(8,128)S(1)}, f32[25,16]{1,0:T(8,128)}, u32[]{:S(2)}) copy-start(f32[25,16]{1,0:T(8,128)} %mul.419) | copy-start | bytes 4804
  100.7 32.9 %copy-start.4 = (bf16[1,1,25,1920]{3,2,1,0:T(8,128)(2,1)S(1)}, bf16[1,1,25,1920]{3,2,1,0:T(8,128)(2,1)}, u32[]{:S(2)}) copy-start(bf16[1,1,25,1920]{3,2,1,0:T(8,128)(2,1)} %param.14) | copy-start | bytes 288004
  100.7 32.9 %copy-start.11 = (f32[1920]{0:T(1024)S(1)}, f32[1920]{0:T(1024)}, u32[]{:S(2)}) copy-start(f32[1920]{0:T(1024)} %get-tuple-element.12) | copy-start | bytes 23044
  101.8 35.2 %copy-start.10 = (f32[1,3,1920]{2,0,1:T(1,128)S(1)}, f32[1,3,1920]{2,0,1:T(1,128)}, u32[]{:S(2)}) copy-start(f32[1,3,1920]{2,0,1:T(1,128)} %get-tuple-element.21) | copy-start | bytes 69124
  121.2 11.9 %all-to-all-start.2 = ((bf16[8,25,240]{2,1,0:T(8,128)(2,1)}), bf16[8,25,240]{2,1,0:T(8,128)(2,1)S(1)}, u32[]{:S(2)}, u32[]{:S(2)}) async-start(bf16[8,25,240]{2,1,0:T(8,128)(2,1)} %convolution_convert_fusion.5), calls=%async_computation.2 | async-start | bytes 262144 | tf_op jit(solution)/shard_map/all_to_all | solution.py:190
  133.6 7.7 %collective-permute-start = (bf16[1,25,1920]{2,1,0:T(8,128)(2,1)S(1)}, bf16[1,25,1920]{2,1,0:T(8,128)(2,1)S(1)}, u32[]{:S(2)}, u32[]{:S(2)}) collective-permute-start(bf16[1,25,1920]{2,1,0:T(8,128)(2,1)S(1)} %fusion.44), channel_id=1, source_target_pairs={{0,8},{8,16},{16,24},{1,9},{9,17},{17,25},{2,10},{10,18},{18,26},{... | collective-permute-start | bytes 288008 | tf_op jit(solution)/shard_map/ppermute | solution.py:15
  161.0 12.6 %copy-start.8 = (bf16[30,1920]{1,0:T(8,128)(2,1)S(1)}, bf16[30,1920]{1,0:T(8,128)(2,1)}, u32[]{:S(2)}) copy-start(bf16[30,1920]{1,0:T(8,128)(2,1)} %get-tuple-element.7) | copy-start | bytes 345604
  165.2 16.6 %all-to-all-start.3 = ((bf16[8,25,3,240]{3,1,2,0:T(8,128)(2,1)}), bf16[8,25,3,240]{3,1,2,0:T(8,128)(2,1)}, u32[]{:S(2)}, u32[]{:S(2)}) async-start(bf16[8,25,3,240]{3,1,2,0:T(8,128)(2,1)} %copy.187), calls=%async_computation.3 | async-start | bytes 786432 | tf_op jit(solution)/shard_map/all_to_all | solution.py:74
  185.2 9.7 %copy-start.2 = (bf16[1,25,3,1920]{3,1,2,0:T(8,128)(2,1)}, bf16[1,25,3,1920]{3,1,2,0:T(8,128)(2,1)S(1)}, u32[]{:S(2)}) copy-start(bf16[1,25,3,1920]{3,1,2,0:T(8,128)(2,1)S(1)} %all_to_all.65) | copy-start | bytes 864004
  195.5 7.1 %slice-start.1 = ((bf16[1,25,3,1920]{3,1,2,0:T(8,128)(2,1)}), bf16[1,25,1,1920]{3,1,2,0:T(8,128)(2,1)S(1)}, s32[]{:S(2)}) async-start(bf16[1,25,3,1920]{3,1,2,0:T(8,128)(2,1)} %copy-done.2), calls=%async_computation.6 | async-start | bytes 245760 | tf_op jit(solution)/shard_map/slice | solution.py:80
  201.5 0.8 copy-start.5
  207.4 25.4 %copy-start.6 = (f32[1,1,25,1920]{3,2,1,0:T(8,128)S(1)}, f32[1,1,25,1920]{3,2,1,0:T(8,128)}, u32[]{:S(2)}) copy-start(f32[1,1,25,1920]{3,2,1,0:T(8,128)} %reshape.1149) | copy-start | bytes 576004
  209.2 33.2 %copy-start.18 = (f32[1920]{0:T(1024)S(1)}, f32[1920]{0:T(1024)}, u32[]{:S(2)}) copy-start(f32[1920]{0:T(1024)} %get-tuple-element.9) | copy-start | bytes 23044
  228.8 10.8 %all-to-all-start.4 = ((bf16[8,25,240]{2,1,0:T(8,128)(2,1)}), bf16[8,25,240]{2,1,0:T(8,128)(2,1)}, u32[]{:S(2)}, u32[]{:S(2)}) async-start(bf16[8,25,240]{2,1,0:T(8,128)(2,1)} %convolution_convert_fusion.4), calls=%async_computation.4 | async-start | bytes 262144 | tf_op jit(solution)/shard_map/all_to_all | solution.py:190
where the time goes:
time: 246 us; the launch traced here: 244 us
  blocking collectives  82.9 us (34%)
  local copies, waits for them, and re-layouts  63.8 us (26%)
  starting transfers between devices  27.2 us (11%)
  matrix products  25.3 us (10%)
  other arithmetic  23.5 us (10%)
  waiting for transfers between devices  20.9 us (8%)
    all_gather x2, blocking collectives, local(): lax.all_gather(normed, 'tp', axis=0, tiled=True)  33.3 us
    all_gather x2, blocking collectives, project_out(): lax.all_gather(attended, 'tp', axis=0, tiled=True)  33.2 us
    all_gather x1, blocking collectives, local(): gated_response = lax.all_gather(activated_part, 'tp', axis=2, tiled=True)  16.4 us
    all_to_all x2, waiting for transfers between devices, local(): lax.all_to_all(projected_cols, 'tp', split_axis=0, concat_axis=2, tiled=T...  12.5 us
    all_to_all x2, starting transfers between devices, attention(): lax.all_to_all(qkv_cols, 'tp', split_axis=0, concat_axis=3, tiled=True)  9.52 us
    all_to_all x2, starting transfers between devices, local(): lax.all_to_all(projected_cols, 'tp', split_axis=0, concat_axis=2, tiled=T...  9.2 us
    dot_general x2, matrix products, attention(): jnp.einsum('ihqk,ikhd->iqhd', probabilities, all_values, preferred_elemen...  7.32 us
    reshape x4, local copies, waits for them, and re-layouts, local(): qkv_cols.reshape(qkv_cols.shape[0], qkv_cols.shape[1], 3, column_width)  6.8 us
  transfers between devices with their start and end apart: 6, of which 4 were waited for; matrix products, arithmetic and copies ran while one was open for 12% of the time, Pallas kernels for 0%

commit v1 on v0

--- a/solution.py
+++ b/solution.py
@@ -71,7 +71,10 @@
 
 
 def attention(qkv_cols, log_scale, cached_keys, cached_values):
-    qkv = lax.all_to_all(qkv_cols, "tp", split_axis=0, concat_axis=3, tiled=True)
+    size = lax.axis_size("tp")
+    pieces = jnp.stack(jnp.split(qkv_cols, size, axis=0), axis=0)
+    pieces = lax.all_to_all(pieces, "tp", split_axis=0, concat_axis=0)
+    qkv = jnp.concatenate(pieces, axis=3)
     images = qkv.shape[0]
     count = qkv.shape[1]
     widened = qkv.astype(jnp.float32)

time: 246 us -> 268 us (1.089)
  local copies, waits for them, and re-layouts: 63.8 us -> 82 us
  waiting for transfers between devices: 20.9 us -> 26.6 us
    another operation x0 -> x20, local copies, waits for them, and re-layouts: none -> 17.4 us  [attention(): pieces = jnp.stack(jnp.split(qkv_cols, size, axis=0), axis=0)]
    unnamed x45 -> x63, local copies, waits for them, and re-layouts: 5.77 us -> 14.5 us
    all_to_all x2, waiting for transfers between devices: 4.72 us -> 11.2 us  [attention(): pieces = lax.all_to_all(pieces, 'tp', split_axis=0, concat_axis=0)]
    all_to_all x4 -> x0, local copies, waits for them, and re-layouts: 4.97 us -> none  [attention(): lax.all_to_all(qkv_cols, 'tp', split_axis=0, concat_axis=3, tiled=True)]
    reshape x4, local copies, waits for them, and re-layouts: 6.8 us -> 3.97 us  [attention(): qkv = jnp.concatenate(pieces, axis=3)]
  transfers between devices with their start and end apart: 6 -> 6, of which waited for: 4 -> 5; matrix products, arithmetic and copies ran while one was open for 12% -> 11% of each run, Pallas kernels for 0% -> 0%
where the time goes in v1:
time: 268 us; the launch traced here: 265 us
  blocking collectives  82.3 us (31%)
  local copies, waits for them, and re-layouts  82 us (31%)
  waiting for transfers between devices  26.6 us (10%)
  starting transfers between devices  25.4 us (9%)
  matrix products  24.3 us (9%)
  other arithmetic  24 us (9%)
    all_gather x2, blocking collectives, local(): lax.all_gather(normed, 'tp', axis=0, tiled=True)  33.3 us
    all_gather x2, blocking collectives, project_out(): lax.all_gather(attended, 'tp', axis=0, tiled=True)  32.6 us
    another operation x20, local copies, waits for them, and re-layouts, attention(): pieces = jnp.stack(jnp.split(qkv_cols, size, axis=0), axis=0)  17.4 us
    all_gather x1, blocking collectives, local(): gated_response = lax.all_gather(activated_part, 'tp', axis=2, tiled=True)  16.4 us
    unnamed x63, local copies, waits for them, and re-layouts  14.5 us
    all_to_all x2, waiting for transfers between devices, local(): lax.all_to_all(projected_cols, 'tp', split_axis=0, concat_axis=2, tiled=T...  11.8 us
    all_to_all x2, waiting for transfers between devices, attention(): pieces = lax.all_to_all(pieces, 'tp', split_axis=0, concat_axis=0)  11.2 us
    all_to_all x2, starting transfers between devices, attention(): pieces = lax.all_to_all(pieces, 'tp', split_axis=0, concat_axis=0)  9.52 us
  transfers between devices with their start and end apart: 6, of which 5 were waited for; matrix products, arithmetic and copies ran while one was open for 11% of the time, Pallas kernels for 0%

profile of v1, /device:TPU:4, one launch (start us, length us, event | category | flops | bytes accessed | tf_op | source)
XLA Modules:
  0.0 265.4 jit_solution(15038861203110491034)
XLA Ops:
  4.4 16.4 %all_gather.15 = bf16[2,8,1920]{1,0,2:T(2,128)(2,1)S(1)} all-gather(bf16[2,8,240]{1,0,2:T(2,128)(2,1)S(1)} %copy.155), channel_id=1, replica_groups=mesh['section'=4,'tp'=8] {'tp'}, dimensions={2}, use_global_device_ids=true | all-gather | bytes 69120 | tf_op jit(solution)/shard_map/all_gather | solution.py:147
  21.5 2.9 %fusion.17 = f32[1,2,8,3,240]{4,2,3,1,0:T(8,128)S(1)} fusion(bf16[1,1920,3,240]{1,3,2,0:T(8,128)(2,1)} %param.21, bf16[2,8,1920,1]{1,0,2,3:T(2,128)(2,1)S(1)} %bitcast.174, f32[3,240]{1,0:T(4,128)S(1)} %bitcast.176), kind=kOutput, calls=%fused_computation.24 | convolution fusion | flops 44248320 | bytes 2875200 | tf_op jit(solution)/shard_map/dot_general | solution.py:151
  25.1 5.1 %all-to-all-start = ((f32[1,2,8,3,240]{4,1,3,0,2:T(2,128)}), f32[1,2,8,3,240]{4,1,3,0,2:T(2,128)}, u32[]{:S(2)}, u32[]{:S(2)}) async-start(f32[1,2,8,3,240]{4,1,3,0,2:T(2,128)} %copy.157), calls=%async_computation | async-start | bytes 98304 | tf_op jit(solution)/shard_map/all_to_all | solution.py:158
  31.2 1.9 convert_reduce_fusion.1
  34.7 1.6 slice_reduce_fusion
  39.5 3.0 %copy.171 = f32[4096,32]{1,0:T(8,128)} copy(f32[4096,32]{0,1:T(8,128)} %param.17) | data formatting | bytes 1048576 | tf_op args[3]
  46.4 17.0 %all_gather.16 = bf16[8,25,1920]{2,1,0:T(8,128)(2,1)S(1)} all-gather(bf16[1,25,1920]{2,1,0:T(8,128)(2,1)S(1)} %fusion.43), channel_id=1, replica_groups=mesh['section'=4,'tp'=8] {'tp'}, dimensions={0}, use_global_device_ids=true | all-gather | bytes 864000 | tf_op jit(solution)/shard_map/all_gather | solution.py:182
  68.6 5.2 %all-to-all-start.1 = ((bf16[8,1,25,3,240]{4,2,3,1,0:T(8,128)(2,1)}), bf16[8,1,25,3,240]{4,2,3,1,0:T(8,128)(2,1)S(1)}, u32[]{:S(2)}, u32[]{:S(2)}) async-start(bf16[8,1,25,3,240]{4,2,3,1,0:T(8,128)(2,1)} %copy.160), calls=%async_computation.1 | async-start | bytes 786432 | tf_op jit(solution)/shard_map/all_to_all | solution.py:76
  76.4 2.9 %gather_fusion.1 = f32[30,32]{1,0:T(8,128)} fusion(f32[4096,32]{1,0:T(8,128)} %copy.171, s32[1024]{0:T(1024)} %get-tuple-element.41), kind=kCustom, calls=%fused_computation.1 | custom fusion | bytes 7800 | tf_op jit(solution)/shard_map/gather | solution.py:47
  79.9 6.4 %all-to-all-done.1 = bf16[8,1,25,3,240]{4,2,3,1,0:T(8,128)(2,1)S(1)} async-done(((bf16[8,1,25,3,240]{4,2,3,1,0:T(8,128)(2,1)}), bf16[8,1,25,3,240]{4,2,3,1,0:T(8,128)(2,1)S(1)}, u32[]{:S(2)}, u32[]{:S(2)}) %all-to-all-start.1) | async-done | bytes 288032 | tf_op jit(solution)/shard_map/all_to_all | solution.py:76
  91.9 1.9 reshape_squeeze.35
  98.1 2.7 %fusion.24 = f32[30,25,55]{2,1,0:T(8,128)S(1)} fusion(f32[1,25,30,64]{3,1,2,0:T(8,128)S(1)} %copy_multiply_fusion.1, f32[1,30,30,64]{3,1,2,0:T(8,128)} %copy.166, f32[25,30,64]{2,1,0:T(8,128)S(1)} %multiply_multiply_fusion.1), kind=kOutput, calls=%fused_computation.31 | convolution fusion | flops 31785600 | bytes 779400 | tf_op jit(solution)/shard_map/iqhd,ikhd->ihqk/dot_general | solution.py:98
  102.0 1.7 copy.163
  103.7 3.5 %fusion.12 = bf16[1,25,30,64]{3,1,2,0:T(8,128)(2,1)} fusion(bf16[1,25,30,64]{3,1,2,0:T(8,128)(2,1)} %copy.163, bf16[1,30,30,64]{3,1,2,0:T(8,128)(2,1)} %copy.162, f32[30,25]{1,0:T(8,128)S(1)} %fusion.75, f32[30,25,55]{2,1,0:T(8,128)S(1)} %fusion.24), kind=kOutput, calls=%fused_computation.19 | convolution fusion | flops 5874954 | bytes 475200 | tf_op jit(solution)/shard_map/ihqk,ikhd->iqhd/dot_general | solution.py:102
  108.5 16.4 %all_gather.17 = bf16[8,25,1920]{2,1,0:T(8,128)(2,1)S(1)} all-gather(bf16[1,25,1920]{2,1,0:T(8,128)(2,1)S(1)} %convert_element_type.264), channel_id=1, replica_groups=mesh['section'=4,'tp'=8] {'tp'}, dimensions={0}, use_global_device_ids=true | all-gather | bytes 864000 | tf_op jit(solution)/shard_map/all_gather | solution.py:110
  124.8 2.3 convolution_convert_fusion.5
  127.1 3.4 %all-to-all-start.2 = ((bf16[8,25,240]{2,1,0:T(8,128)(2,1)}), bf16[8,25,240]{2,1,0:T(8,128)(2,1)S(1)}, u32[]{:S(2)}, u32[]{:S(2)}) async-start(bf16[8,25,240]{2,1,0:T(8,128)(2,1)} %convolution_convert_fusion.5), calls=%async_computation.2 | async-start | bytes 262144 | tf_op jit(solution)/shard_map/all_to_all | solution.py:193
  131.4 5.8 %all-to-all-done.2 = bf16[8,25,240]{2,1,0:T(8,128)(2,1)S(1)} async-done(((bf16[8,25,240]{2,1,0:T(8,128)(2,1)}), bf16[8,25,240]{2,1,0:T(8,128)(2,1)S(1)}, u32[]{:S(2)}, u32[]{:S(2)}) %all-to-all-start.2) | async-done | bytes 96032 | tf_op jit(solution)/shard_map/all_to_all | solution.py:193
  137.6 3.4 %collective-permute-start = (bf16[1,25,1920]{2,1,0:T(8,128)(2,1)S(1)}, bf16[1,25,1920]{2,1,0:T(8,128)(2,1)S(1)}, u32[]{:S(2)}, u32[]{:S(2)}) collective-permute-start(bf16[1,25,1920]{2,1,0:T(8,128)(2,1)S(1)} %fusion.44), channel_id=1, source_target_pairs={{0,8},{8,16},{16,24},{1,9},{9,17},{17,25},{2,10},{10,18},{18,26},{... | collective-permute-start | bytes 288008 | tf_op jit(solution)/shard_map/ppermute | solution.py:15
  141.6 3.6 %collective-permute-done = bf16[1,25,1920]{2,1,0:T(8,128)(2,1)S(1)} collective-permute-done((bf16[1,25,1920]{2,1,0:T(8,128)(2,1)S(1)}, bf16[1,25,1920]{2,1,0:T(8,128)(2,1)S(1)}, u32[]{:S(2)}, u32[]{:S(2)}) %collective-permute-start) | collective-permute-done | bytes 96032 | tf_op jit(solution)/shard_map/ppermute | solution.py:15
  146.9 16.3 %all_gather.18 = bf16[8,25,1920]{2,1,0:T(8,128)(2,1)S(1)} all-gather(bf16[1,25,1920]{2,1,0:T(8,128)(2,1)S(1)} %add_convert_fusion.1), channel_id=1, replica_groups=mesh['section'=4,'tp'=8] {'tp'}, dimensions={0}, use_global_device_ids=true | all-gather | bytes 864000 | tf_op jit(solution)/shard_map/all_gather | solution.py:182
  166.6 1.5 stack.75
  168.1 1.5 stack.76
  169.6 1.5 stack.77
  171.2 1.5 stack.78
  172.7 1.5 stack.79
  175.1 1.5 stack.81
  176.6 1.4 constant_dynamic-update-slice_fusion.14
  178.1 1.4 constant_dynamic-update-slice_fusion.13
  180.9 1.4 constant_dynamic-update-slice_fusion.11
  182.4 1.4 constant_dynamic-update-slice_fusion.10
  185.9 1.8 copy.177
  187.7 4.3 %all-to-all-start.3 = ((bf16[8,1,25,3,240]{4,2,3,1,0:T(8,128)(2,1)}), bf16[8,1,25,3,240]{4,2,3,1,0:T(8,128)(2,1)}, u32[]{:S(2)}, u32[]{:S(2)}) async-start(bf16[8,1,25,3,240]{4,2,3,1,0:T(8,128)(2,1)} %copy.177), calls=%async_computation.3 | async-start | bytes 786432 | tf_op jit(solution)/shard_map/all_to_all | solution.py:76
  192.0 2.0 reshape.1161
  194.0 2.1 copy.183
  197.0 1.7 copy.179
  199.6 4.7 %all-to-all-done.3 = bf16[8,1,25,3,240]{4,2,3,1,0:T(8,128)(2,1)} async-done(((bf16[8,1,25,3,240]{4,2,3,1,0:T(8,128)(2,1)}), bf16[8,1,25,3,240]{4,2,3,1,0:T(8,128)(2,1)}, u32[]{:S(2)}, u32[]{:S(2)}) %all-to-all-start.3) | async-done | bytes 288032 | tf_op jit(solution)/shard_map/all_to_all | solution.py:76
  204.4 1.9 copy.178
  209.3 1.9 mul.431
  212.4 1.9 reshape_squeeze.39
  214.3 1.9 reshape_squeeze.40
  220.0 2.7 %fusion.27 = f32[30,25,55]{2,1,0:T(8,128)S(1)} fusion(f32[1,25,30,64]{3,1,2,0:T(8,128)S(1)} %copy_multiply_fusion, f32[1,30,30,64]{3,1,2,0:T(8,128)} %copy.183, f32[25,30,64]{2,1,0:T(8,128)S(1)} %multiply_multiply_fusion), kind=kOutput, calls=%fused_computation.35 | convolution fusion | flops 31785600 | bytes 779400 | tf_op jit(solution)/shard_map/iqhd,ikhd->ihqk/dot_general | solution.py:98
  224.8 3.8 %fusion.13 = bf16[1,25,30,64]{3,1,2,0:T(8,128)(2,1)} fusion(bf16[1,25,30,64]{3,1,2,0:T(8,128)(2,1)} %copy.180, bf16[1,30,30,64]{3,1,2,0:T(8,128)(2,1)} %copy.179, f32[30,25]{1,0:T(8,128)S(1)} %fusion.77, f32[30,25,55]{2,1,0:T(8,128)} %copy-done.5), kind=kOutput, calls=%fused_computation.20 | convolution fusion | flops 5874954 | bytes 475200 | tf_op jit(solution)/shard_map/ihqk,ikhd->iqhd/dot_general | solution.py:102
  228.6 1.7 copy.185
  231.5 16.2 %all_gather.19 = bf16[8,25,1920]{2,1,0:T(8,128)(2,1)S(1)} all-gather(bf16[1,25,1920]{2,1,0:T(8,128)(2,1)S(1)} %convert_element_type.289), channel_id=1, replica_groups=mesh['section'=4,'tp'=8] {'tp'}, dimensions={0}, use_global_device_ids=true | all-gather | bytes 864000 | tf_op jit(solution)/shard_map/all_gather | solution.py:110
  247.7 2.3 convolution_convert_fusion.4
  250.0 4.0 %all-to-all-start.4 = ((bf16[8,25,240]{2,1,0:T(8,128)(2,1)}), bf16[8,25,240]{2,1,0:T(8,128)(2,1)}, u32[]{:S(2)}, u32[]{:S(2)}) async-start(bf16[8,25,240]{2,1,0:T(8,128)(2,1)} %convolution_convert_fusion.4), calls=%async_computation.4 | async-start | bytes 262144 | tf_op jit(solution)/shard_map/all_to_all | solution.py:193
  254.7 6.1 %all-to-all-done.4 = bf16[8,25,240]{2,1,0:T(8,128)(2,1)} async-done(((bf16[8,25,240]{2,1,0:T(8,128)(2,1)}), bf16[8,25,240]{2,1,0:T(8,128)(2,1)}, u32[]{:S(2)}, u32[]{:S(2)}) %all-to-all-start.4) | async-done | bytes 96032 | tf_op jit(solution)/shard_map/all_to_all | solution.py:193
  (177 shorter events, 65.5 us)
Async XLA Ops:
  0.0 63.4 %copy-start = (bf16[1,1920,3,240]{1,3,2,0:T(8,128)(2,1)S(1)}, bf16[1,1920,3,240]{1,3,2,0:T(8,128)(2,1)}, u32[]{:S(2)}) copy-start(bf16[1,1920,3,240]{1,3,2,0:T(8,128)(2,1)} %param.23) | copy-start | bytes 8294404
  2.2 28.1 %copy-start.3 = (bf16[1,1,25,1920]{3,2,1,0:T(8,128)(2,1)S(1)}, bf16[1,1,25,1920]{3,2,1,0:T(8,128)(2,1)}, u32[]{:S(2)}) copy-start(bf16[1,1,25,1920]{3,2,1,0:T(8,128)(2,1)} %param.14) | copy-start | bytes 288004
  4.1 27.1 %copy-start.7 = (bf16[1,2,1,30,1920]{4,1,3,2,0:T(2,128)(2,1)S(1)}, bf16[1,2,1,30,1920]{4,1,3,2,0:T(2,128)(2,1)}, u32[]{:S(2)}) copy-start(bf16[1,2,1,30,1920]{4,1,3,2,0:T(2,128)(2,1)} %param.26) | copy-start | bytes 691204
  20.8 13.9 %copy-start.8 = (bf16[1,2,1,30,1920]{4,1,3,2,0:T(2,128)(2,1)S(1)}, bf16[1,2,1,30,1920]{4,1,3,2,0:T(2,128)(2,1)}, u32[]{:S(2)}) copy-start(bf16[1,2,1,30,1920]{4,1,3,2,0:T(2,128)(2,1)} %param.27) | copy-start | bytes 691204
  25.1 18.9 %all-to-all-start = ((f32[1,2,8,3,240]{4,1,3,0,2:T(2,128)}), f32[1,2,8,3,240]{4,1,3,0,2:T(2,128)}, u32[]{:S(2)}, u32[]{:S(2)}) async-start(f32[1,2,8,3,240]{4,1,3,0,2:T(2,128)} %copy.157), calls=%async_computation | async-start | bytes 98304 | tf_op jit(solution)/shard_map/all_to_all | solution.py:158
  30.4 2.7 %copy-start.20 = (f32[25]{0:T(128)}, f32[25]{0:T(128)S(1)}, u32[]{:S(2)}) copy-start(f32[25]{0:T(128)S(1)} %broadcast_multiply_fusion.4) | copy-start | bytes 304
  38.5 4.7 %copy-start.10 = (f32[5,5,3,3]{1,0,3,2:T(8,128)S(1)}, f32[5,5,3,3]{1,0,3,2:T(8,128)}, u32[]{:S(2)}) copy-start(f32[5,5,3,3]{1,0,3,2:T(8,128)} %broadcast_multiply_fusion.1) | copy-start | bytes 2704
  45.6 91.9 %copy-start.12 = (f32[1920]{0:T(1024)}, f32[1920]{0:T(1024)S(1)}, u32[]{:S(2)}) copy-start(f32[1920]{0:T(1024)S(1)} %get-tuple-element.12) | copy-start | bytes 23044
  68.6 17.7 %all-to-all-start.1 = ((bf16[8,1,25,3,240]{4,2,3,1,0:T(8,128)(2,1)}), bf16[8,1,25,3,240]{4,2,3,1,0:T(8,128)(2,1)S(1)}, u32[]{:S(2)}, u32[]{:S(2)}) async-start(bf16[8,1,25,3,240]{4,2,3,1,0:T(8,128)(2,1)} %copy.160), calls=%async_computation.1 | async-start | bytes 786432 | tf_op jit(solution)/shard_map/all_to_all | solution.py:76
  79.9 16.9 %copy-start.21 = (f32[30]{0:T(128)}, f32[30]{0:T(128)S(1)}, u32[]{:S(2)}) copy-start(f32[30]{0:T(128)S(1)} %exponential_bitcast_fusion) | copy-start | bytes 364
  87.0 8.1 %copy-start.1 = (bf16[1,25,3,1920]{3,1,2,0:T(8,128)(2,1)}, bf16[1,25,3,1920]{3,1,2,0:T(8,128)(2,1)S(1)}, u32[]{:S(2)}) copy-start(bf16[1,25,3,1920]{3,1,2,0:T(8,128)(2,1)S(1)} %reshape.1149) | copy-start | bytes 864004
  95.7 5.3 %slice-start = ((bf16[1,25,3,1920]{3,1,2,0:T(8,128)(2,1)}), bf16[1,25,1,1920]{3,1,2,0:T(8,128)(2,1)S(1)}, s32[]{:S(2)}) async-start(bf16[1,25,3,1920]{3,1,2,0:T(8,128)(2,1)} %copy-done.1), calls=%async_computation.5 | async-start | bytes 245760 | tf_op jit(solution)/shard_map/slice | solution.py:83
  107.1 23.4 %copy-start.14 = (f32[30,32]{1,0:T(8,128)S(1)}, f32[30,32]{1,0:T(8,128)}, u32[]{:S(2)}) copy-start(f32[30,32]{1,0:T(8,128)} %gather_fusion.1) | copy-start | bytes 11524
  107.1 23.4 %copy-start.15 = (f32[25,9]{1,0:T(8,128)S(1)}, f32[25,9]{1,0:T(8,128)}, u32[]{:S(2)}) copy-start(f32[25,9]{1,0:T(8,128)} %copy.174) | copy-start | bytes 2704
  107.1 23.4 %copy-start.16 = (f32[25,4]{1,0:T(8,128)S(1)}, f32[25,4]{1,0:T(8,128)}, u32[]{:S(2)}) copy-start(f32[25,4]{1,0:T(8,128)} %copy.173) | copy-start | bytes 1204
  107.1 23.4 %copy-start.17 = (f32[25,1]{1,0:T(8,128)S(1)}, f32[25,1]{1,0:T(8,128)}, u32[]{:S(2)}) copy-start(f32[25,1]{1,0:T(8,128)} %copy.172) | copy-start | bytes 304
  107.1 23.4 %copy-start.18 = (f32[25,16]{1,0:T(8,128)S(1)}, f32[25,16]{1,0:T(8,128)}, u32[]{:S(2)}) copy-start(f32[25,16]{1,0:T(8,128)} %mul.419) | copy-start | bytes 4804
  107.2 30.4 %copy-start.4 = (bf16[1,1,25,1920]{3,2,1,0:T(8,128)(2,1)S(1)}, bf16[1,1,25,1920]{3,2,1,0:T(8,128)(2,1)}, u32[]{:S(2)}) copy-start(bf16[1,1,25,1920]{3,2,1,0:T(8,128)(2,1)} %param.14) | copy-start | bytes 288004
  108.3 32.7 %copy-start.11 = (f32[1,3,1920]{2,0,1:T(1,128)S(1)}, f32[1,3,1920]{2,0,1:T(1,128)}, u32[]{:S(2)}) copy-start(f32[1,3,1920]{2,0,1:T(1,128)} %get-tuple-element.37) | copy-start | bytes 69124
  127.1 10.1 %all-to-all-start.2 = ((bf16[8,25,240]{2,1,0:T(8,128)(2,1)}), bf16[8,25,240]{2,1,0:T(8,128)(2,1)S(1)}, u32[]{:S(2)}, u32[]{:S(2)}) async-start(bf16[8,25,240]{2,1,0:T(8,128)(2,1)} %convolution_convert_fusion.5), calls=%async_computation.2 | async-start | bytes 262144 | tf_op jit(solution)/shard_map/all_to_all | solution.py:193
  137.6 7.7 %collective-permute-start = (bf16[1,25,1920]{2,1,0:T(8,128)(2,1)S(1)}, bf16[1,25,1920]{2,1,0:T(8,128)(2,1)S(1)}, u32[]{:S(2)}, u32[]{:S(2)}) collective-permute-start(bf16[1,25,1920]{2,1,0:T(8,128)(2,1)S(1)} %fusion.44), channel_id=1, source_target_pairs={{0,8},{8,16},{16,24},{1,9},{9,17},{17,25},{2,10},{10,18},{18,26},{... | collective-permute-start | bytes 288008 | tf_op jit(solution)/shard_map/ppermute | solution.py:15
  164.3 31.8 %copy-start.9 = (bf16[30,1920]{1,0:T(8,128)(2,1)S(1)}, bf16[30,1920]{1,0:T(8,128)(2,1)}, u32[]{:S(2)}) copy-start(bf16[30,1920]{1,0:T(8,128)(2,1)} %get-tuple-element.7) | copy-start | bytes 345604
  187.7 16.6 %all-to-all-start.3 = ((bf16[8,1,25,3,240]{4,2,3,1,0:T(8,128)(2,1)}), bf16[8,1,25,3,240]{4,2,3,1,0:T(8,128)(2,1)}, u32[]{:S(2)}, u32[]{:S(2)}) async-start(bf16[8,1,25,3,240]{4,2,3,1,0:T(8,128)(2,1)} %copy.177), calls=%async_computation.3 | async-start | bytes 786432 | tf_op jit(solution)/shard_map/all_to_all | solution.py:76
  207.7 9.7 %copy-start.2 = (bf16[1,25,3,1920]{3,1,2,0:T(8,128)(2,1)}, bf16[1,25,3,1920]{3,1,2,0:T(8,128)(2,1)S(1)}, u32[]{:S(2)}) copy-start(bf16[1,25,3,1920]{3,1,2,0:T(8,128)(2,1)S(1)} %reshape.1155) | copy-start | bytes 864004
  207.8 11.1 %copy-start.22 = (f32[30]{0:T(128)S(1)}, f32[30]{0:T(128)}, u32[]{:S(2)}) copy-start(f32[30]{0:T(128)} %copy-done.21) | copy-start | bytes 364
  217.4 6.4 %slice-start.1 = ((bf16[1,25,3,1920]{3,1,2,0:T(8,128)(2,1)}), bf16[1,25,1,1920]{3,1,2,0:T(8,128)(2,1)S(1)}, s32[]{:S(2)}) async-start(bf16[1,25,3,1920]{3,1,2,0:T(8,128)(2,1)} %copy-done.2), calls=%async_computation.6 | async-start | bytes 245760 | tf_op jit(solution)/shard_map/slice | solution.py:83
  222.7 0.8 copy-start.5
  228.6 25.4 %copy-start.6 = (f32[1,1,25,1920]{3,2,1,0:T(8,128)S(1)}, f32[1,1,25,1920]{3,2,1,0:T(8,128)}, u32[]{:S(2)}) copy-start(f32[1,1,25,1920]{3,2,1,0:T(8,128)} %reshape.1190) | copy-start | bytes 576004
  228.6 25.4 %copy-start.13 = (f32[1920]{0:T(1024)S(1)}, f32[1920]{0:T(1024)}, u32[]{:S(2)}) copy-start(f32[1920]{0:T(1024)} %copy-done.12) | copy-start | bytes 23044
  230.4 33.2 %copy-start.19 = (f32[1920]{0:T(1024)S(1)}, f32[1920]{0:T(1024)}, u32[]{:S(2)}) copy-start(f32[1920]{0:T(1024)} %get-tuple-element.9) | copy-start | bytes 23044
  250.0 10.8 %all-to-all-start.4 = ((bf16[8,25,240]{2,1,0:T(8,128)(2,1)}), bf16[8,25,240]{2,1,0:T(8,128)(2,1)}, u32[]{:S(2)}, u32[]{:S(2)}) async-start(bf16[8,25,240]{2,1,0:T(8,128)(2,1)} %convolution_convert_fusion.4), calls=%async_computation.4 | async-start | bytes 262144 | tf_op jit(solution)/shard_map/all_to_all | solution.py:193
